TPU v7x, 32 devices: a whole 2x2x4 slice. The times are simulated.
32 devices in a mesh: gx: 4 (over y, core), yz: 8 (over z, x).
Axes of the slice: x: 2, y: 2, z: 4, core: 2. Of those that a mesh axis runs over, the one named last changes fastest.
Arguments:
- orbitals: bfloat16 [4, 8, 9, 128, 256], P('gx', 'yz'), may hold values from -0.125 to 0.125
- potential: float32 [4, 8, 256], P('gx', 'yz'), may hold values from 0.25 to 4
- density: bfloat16 [4, 8, 9, 128, 128], P('gx', 'yz'), may hold values from -0.1 to 0.6
- pattern: int32 [4, 8, 9], P('gx', 'yz'), may hold values 0 or 1
Outputs:
- hamiltonian: float32 [4, 8, 9, 128, 128], P('gx', 'yz')
- margin: float32 [4, 8, 9, 128, 128], P('gx', 'yz')
- purified: float32 [4, 8, 9, 128, 128], P('gx', 'yz')
All inputs are finite; a program needn't handle non-finite values. No bound on the sum of `pattern` on one device may be relied on, other than what follows from the above.
Results may differ from a plain program's by a relative error of at most 0.0068.
Values may be sent and summed in bfloat16 or wider, within the bound.
A program may use at most 64 MiB of HBM per device.

v0:
```python
import jax
import jax.numpy as jnp
from jax import lax
from jax.sharding import PartitionSpec as P


def from_behind(value, axis, by):
    count = lax.axis_size(axis)
    return lax.ppermute(value, axis, [(i, (i + by) % count) for i in range(count)])


def extended(block, sides, width):
    for axis, dim in sides:
        count = lax.axis_size(axis)
        forward = [(i, i + 1) for i in range(count - 1)]
        forward.append((count - 1, 0))
        backward = [(target, source) for source, target in forward]
        low = lax.ppermute(
            lax.slice_in_dim(block, block.shape[dim] - width, None, axis=dim), axis, forward
        )
        high = lax.ppermute(lax.slice_in_dim(block, 0, width, axis=dim), axis, backward)
        block = jnp.concatenate([low, block, high], axis=dim)
    return block


def offset_of(index):
    return (index // 3 - 1, index % 3 - 1)


def slot_for(shift_x, shift_y):
    return (shift_x + 1) * 3 + shift_y + 1


def line_steps(values):
    lead = values.shape[:-1]
    lines = values.astype(jnp.float32).reshape(lead + (values.shape[-1] // 128, 128))
    forward = lines[..., 1:] - lines[..., :-1]
    padded = jnp.concatenate(
        [forward, jnp.zeros(lead + (lines.shape[-2], 1), jnp.float32)], axis=-1
    )
    return padded.reshape(values.shape).astype(jnp.bfloat16)


def reachable(slot):
    ka, kb = offset_of(slot)
    found = []
    for target in range(9):
        pa, pb = offset_of(target)
        if abs(ka - pa) <= 1 and abs(kb - pb) <= 1:
            found.append(target)
    return found


def package(blocks, slot, targets):
    rows = []
    ka, kb = offset_of(slot)
    for target in targets:
        pa, pb = offset_of(target)
        la, lb = (ka - pa, kb - pb)
        rows.append(blocks[:, slot, :, slot_for(la, lb), :])
    return jnp.stack(rows, axis=1)


def spread(parcel, targets, width):
    rows = [jnp.zeros((2, width, width), jnp.float32)] * 9
    for place, target in enumerate(targets):
        rows[target] = parcel[:, place]
    return jnp.stack(rows, axis=1)


def block_product(left, near, keep):
    terms = [None] * 9
    for first in range(9):
        fa, fb = offset_of(first)
        row = jnp.einsum(
            "ij,pjk->pik", left[first], near[1 + fa, 1 + fb], preferred_element_type=jnp.float32
        )
        for second in range(9):
            sa, sb = offset_of(second)
            oa, ob = (fa + sa, fb + sb)
            if abs(oa) > 1 or abs(ob) > 1:
                continue
            target = slot_for(oa, ob)
            terms[target] = row[second] if terms[target] is None else terms[target] + row[second]
    return jnp.stack(terms) * keep


def body(orbitals, potential, density, pattern):
    values = orbitals[0, 0]
    width = values.shape[1]
    cells = values.shape[2]
    keep = pattern[0, 0].astype(jnp.float32)[:, None, None]
    flat = values.reshape(9 * width, cells)
    weighted = (flat.astype(jnp.float32) * potential[0, 0][None, :]).astype(jnp.bfloat16)
    steps = line_steps(flat)
    s_all = jnp.einsum("ig,jg->ij", flat, flat, preferred_element_type=jnp.float32)
    h_all = jnp.einsum("ig,jg->ij", flat, weighted, preferred_element_type=jnp.float32)
    h_all = h_all + 0.5 * jnp.einsum("ig,jg->ij", steps, steps, preferred_element_type=jnp.float32)
    blocks = jnp.stack([h_all, s_all]).reshape(2, 9, width, 9, width)
    total = jnp.zeros((2, 9, width, width), jnp.float32)
    for slot in range(9):
        ka, kb = offset_of(slot)
        targets = reachable(slot)
        parcel = package(blocks, slot, targets)
        if ka != 0:
            parcel = from_behind(parcel, "gx", -ka)
        if kb != 0:
            parcel = from_behind(parcel, "yz", -kb)
        total = total + spread(parcel, targets, width)
    hamiltonian = total[0] * keep
    margin = total[1] * keep
    current = density[0, 0] * pattern[0, 0].astype(jnp.bfloat16)[:, None, None]
    margin_low = margin.astype(jnp.bfloat16)
    margin_near = extended(margin_low[None, None], (("gx", 0), ("yz", 1)), 1)
    purified = jnp.zeros(margin.shape, jnp.float32)
    for step in range(2):
        first = block_product(current, margin_near, keep)
        first_low = first.astype(jnp.bfloat16)
        density_near = extended(current[None, None], (("gx", 0), ("yz", 1)), 1)
        third = block_product(first_low, density_near, keep)
        third_low = third.astype(jnp.bfloat16)
        cubic_near = extended(third_low[None, None], (("gx", 0), ("yz", 1)), 1)
        fifth = block_product(first_low, cubic_near, keep)
        purified = 3.0 * third - 2.0 * fifth
        current = purified.astype(jnp.bfloat16)
    return (hamiltonian[None, None], margin[None, None], purified[None, None])


def solution(mesh):
    placed = (
        P("gx", "yz", None, None, None),
        P("gx", "yz", None),
        P("gx", "yz", None, None, None),
        P("gx", "yz", None),
    )
    return jax.shard_map(
        body,
        mesh=mesh,
        in_specs=placed,
        out_specs=(
            P("gx", "yz", None, None, None),
            P("gx", "yz", None, None, None),
            P("gx", "yz", None, None, None),
        ),
        check_vma=False,
    )
```

profile of v0, /device:TPU:1, one launch (start us, length us, event | category | flops | bytes accessed | tf_op | source)
XLA Modules:
  0.0 377.2 jit_solution(16746921176505771369)
XLA Ops:
  0.6 1.9 reshape.656
  2.5 3.3 convolution_bitcast_fusion.2
  5.8 1.4 fusion.47
  8.5 3.2 fusion.1
  11.7 7.9 %reshape.695 = f32[1,9,128,9,128]{2,1,4,3,0:T(8,128)} reshape(f32[1152,1152]{0,1:T(8,128)} %fusion.1) | data formatting | bytes 10616832 | tf_op jit(solution)/shard_map/stack | solution.py:99
  19.6 8.7 %copy.161 = f32[1,9,128,9,128]{4,2,3,1,0:T(8,128)} copy(f32[1,9,128,9,128]{2,1,4,3,0:T(8,128)} %reshape.695) | data formatting | bytes 10616832 | tf_op jit(solution)/shard_map/stack | solution.py:99
  28.3 1.0 constant_dynamic-update-slice_fusion.32
  29.4 1.5 copy-done
  30.9 1.1 constant_dynamic-update-slice_fusion.31
  33.0 2.1 collective-permute-start.5
  35.1 3.1 collective-permute-start.6
  38.2 2.2 collective-permute-start.2
  40.7 1.8 collective-permute-start.3
  43.2 25.0 %collective-permute-done.5 = f32[2,6,128,128]{3,2,0,1:T(8,128)S(1)} collective-permute-done((f32[2,6,128,128]{3,2,0,1:T(8,128)S(1)}, f32[2,6,128,128]{3,2,0,1:T(8,128)S(1)}, u32[]{:S(2)}, u32[]{:S(2)}) %collective-permute-start.5) | collective-permute-done | bytes 786464 | tf_op jit(solution)/shard_map/ppermute | solution.py:9
  68.1 1.5 collective-permute-start.10
  69.8 1.2 collective-permute-start
  71.0 2.2 collective-permute-start.8
  73.2 3.1 collective-permute-start.4
  76.4 7.0 %collective-permute-done.10 = f32[2,4,128,128]{3,2,0,1:T(8,128)S(1)} collective-permute-done((f32[2,4,128,128]{3,2,0,1:T(8,128)S(1)}, f32[2,4,128,128]{3,2,0,1:T(8,128)S(1)}, u32[]{:S(2)}, u32[]{:S(2)}) %collective-permute-start.10) | collective-permute-done | bytes 524320 | tf_op jit(solution)/shard_map/ppermute | solution.py:9
  83.4 5.2 %collective-permute-start.11 = (f32[2,4,128,128]{3,2,0,1:T(8,128)S(1)}, f32[2,4,128,128]{3,2,0,1:T(8,128)S(1)}, u32[]{:S(2)}, u32[]{:S(2)}) collective-permute-start(f32[2,4,128,128]{3,2,0,1:T(8,128)S(1)} %collective-permute-done.10), channel_id=1, source_target_pairs={{0,7},{1,0},{2,1},{3,2},{4,3},{5,4},{6,5},{7,6},{8,15},{9,8},{10,9... | collective-permute-start | bytes 1572872 | tf_op jit(solution)/shard_map/ppermute | solution.py:9
  88.6 18.6 %collective-permute-done.8 = f32[2,4,128,128]{3,2,0,1:T(8,128)S(1)} collective-permute-done((f32[2,4,128,128]{3,2,0,1:T(8,128)S(1)}, f32[2,4,128,128]{3,2,0,1:T(8,128)S(1)}, u32[]{:S(2)}, u32[]{:S(2)}) %collective-permute-start.8) | collective-permute-done | bytes 524320 | tf_op jit(solution)/shard_map/ppermute | solution.py:9
  107.2 2.0 collective-permute-start.1
  109.5 14.7 %collective-permute-done.1 = f32[2,4,128,128]{3,2,0,1:T(8,128)S(1)} collective-permute-done((f32[2,4,128,128]{3,2,0,1:T(8,128)S(1)}, f32[2,4,128,128]{3,2,0,1:T(8,128)S(1)}, u32[]{:S(2)}, u32[]{:S(2)}) %collective-permute-start.1) | collective-permute-done | bytes 524320 | tf_op jit(solution)/shard_map/ppermute | solution.py:9
  125.3 1.2 fusion.46
  127.9 1.6 collective-permute-start.12
  129.7 2.3 collective-permute-done.15
  132.1 4.9 %collective-permute-done.16 = bf16[1,1,9,128,128]{4,3,2,1,0:T(8,128)(2,1)S(1)} collective-permute-done((bf16[1,1,9,128,128]{4,3,2,1,0:T(8,128)(2,1)S(1)}, bf16[1,1,9,128,128]{4,3,2,1,0:T(8,128)(2,1)S(1)}, u32[]{:S(2)}, u32[]{:S(2)}) %collective-permute-start.16) | collective-permute-done | bytes 294944 | tf_op jit(solution)/shard_map/ppermute | solution.py:21
  137.2 1.2 collective-permute-done.12
  138.4 4.4 %collective-permute-done.13 = bf16[1,1,9,128,128]{3,4,2,1,0:T(8,128)(2,1)S(1)} collective-permute-done((bf16[1,1,9,128,128]{3,4,2,1,0:T(8,128)(2,1)S(1)}, bf16[1,1,9,128,128]{3,4,2,1,0:T(8,128)(2,1)S(1)}, u32[]{:S(2)}, u32[]{:S(2)}) %collective-permute-start.13) | collective-permute-done | bytes 294944 | tf_op jit(solution)/shard_map/ppermute | solution.py:21
  143.0 4.1 %collective-permute-start.19 = (bf16[3,1,9,128,128]{3,4,2,1,0:T(8,128)(2,1)S(1)}, bf16[3,1,9,128,128]{3,4,2,1,0:T(8,128)(2,1)S(1)}, u32[]{:S(2)}, u32[]{:S(2)}) collective-permute-start(bf16[3,1,9,128,128]{3,4,2,1,0:T(8,128)(2,1)S(1)} %pad_maximum_fusion.2), channel_id=1, source_target_pairs={{1,0},{2,1},{3,2},{4,3},{5,4},{6,5},{7,6},{0,7},{9,8},{10,9},{11,1... | collective-permute-start | bytes 2654216 | tf_op jit(solution)/shard_map/ppermute | solution.py:21
  148.1 46.4 %collective-permute-done.17 = bf16[3,1,9,128,128]{4,3,2,1,0:T(8,128)(2,1)S(1)} collective-permute-done((bf16[3,1,9,128,128]{4,3,2,1,0:T(8,128)(2,1)S(1)}, bf16[3,1,9,128,128]{4,3,2,1,0:T(8,128)(2,1)S(1)}, u32[]{:S(2)}, u32[]{:S(2)}) %collective-permute-start.17) | collective-permute-done | bytes 884768 | tf_op jit(solution)/shard_map/ppermute | solution.py:18
  195.0 23.3 %collective-permute-done.18 = bf16[3,1,9,128,128]{4,3,2,1,0:T(8,128)(2,1)S(1)} collective-permute-done((bf16[3,1,9,128,128]{4,3,2,1,0:T(8,128)(2,1)S(1)}, bf16[3,1,9,128,128]{4,3,2,1,0:T(8,128)(2,1)S(1)}, u32[]{:S(2)}, u32[]{:S(2)}) %collective-permute-start.18) | collective-permute-done | bytes 884768 | tf_op jit(solution)/shard_map/ppermute | solution.py:21
  222.9 4.7 %collective-permute-done.20 = bf16[1,1,9,128,128]{4,3,2,1,0:T(8,128)(2,1)S(1)} collective-permute-done((bf16[1,1,9,128,128]{4,3,2,1,0:T(8,128)(2,1)S(1)}, bf16[1,1,9,128,128]{4,3,2,1,0:T(8,128)(2,1)S(1)}, u32[]{:S(2)}, u32[]{:S(2)}) %collective-permute-start.20) | collective-permute-done | bytes 294944 | tf_op jit(solution)/shard_map/ppermute | solution.py:18
  227.6 3.7 collective-permute-done.21
  231.8 4.2 %collective-permute-start.23 = (bf16[3,1,9,128,128]{4,3,2,1,0:T(8,128)(2,1)S(1)}, bf16[3,1,9,128,128]{4,3,2,1,0:T(8,128)(2,1)S(1)}, u32[]{:S(2)}, u32[]{:S(2)}) collective-permute-start(bf16[3,1,9,128,128]{4,3,2,1,0:T(8,128)(2,1)S(1)} %pad_maximum_fusion.4), channel_id=1, source_target_pairs={{1,0},{2,1},{3,2},{4,3},{5,4},{6,5},{7,6},{0,7},{9,8},{10,9},{11,1... | collective-permute-start | bytes 2654216 | tf_op jit(solution)/shard_map/ppermute | solution.py:21
  236.5 33.3 %collective-permute-done.22 = bf16[3,1,9,128,128]{4,3,2,1,0:T(8,128)(2,1)S(1)} collective-permute-done((bf16[3,1,9,128,128]{4,3,2,1,0:T(8,128)(2,1)S(1)}, bf16[3,1,9,128,128]{4,3,2,1,0:T(8,128)(2,1)S(1)}, u32[]{:S(2)}, u32[]{:S(2)}) %collective-permute-start.22) | collective-permute-done | bytes 884768 | tf_op jit(solution)/shard_map/ppermute | solution.py:18
  270.2 1.8 collective-permute-done.23
  277.1 2.1 collective-permute-done.24
  279.2 3.7 collective-permute-done.25
  283.5 4.1 %collective-permute-start.27 = (bf16[3,1,9,128,128]{4,3,2,1,0:T(8,128)(2,1)S(1)}, bf16[3,1,9,128,128]{4,3,2,1,0:T(8,128)(2,1)S(1)}, u32[]{:S(2)}, u32[]{:S(2)}) collective-permute-start(bf16[3,1,9,128,128]{4,3,2,1,0:T(8,128)(2,1)S(1)} %pad_maximum_fusion.5), channel_id=1, source_target_pairs={{1,0},{2,1},{3,2},{4,3},{5,4},{6,5},{7,6},{0,7},{9,8},{10,9},{11,1... | collective-permute-start | bytes 2654216 | tf_op jit(solution)/shard_map/ppermute | solution.py:21
  288.1 33.0 %collective-permute-done.26 = bf16[3,1,9,128,128]{4,3,2,1,0:T(8,128)(2,1)S(1)} collective-permute-done((bf16[3,1,9,128,128]{4,3,2,1,0:T(8,128)(2,1)S(1)}, bf16[3,1,9,128,128]{4,3,2,1,0:T(8,128)(2,1)S(1)}, u32[]{:S(2)}, u32[]{:S(2)}) %collective-permute-start.26) | collective-permute-done | bytes 884768 | tf_op jit(solution)/shard_map/ppermute | solution.py:18
  321.6 1.8 collective-permute-done.27
  324.8 1.2 collective-permute-start.28
  326.1 4.7 %collective-permute-done.28 = bf16[1,1,9,128,128]{4,3,2,1,0:T(8,128)(2,1)S(1)} collective-permute-done((bf16[1,1,9,128,128]{4,3,2,1,0:T(8,128)(2,1)S(1)}, bf16[1,1,9,128,128]{4,3,2,1,0:T(8,128)(2,1)S(1)}, u32[]{:S(2)}, u32[]{:S(2)}) %collective-permute-start.28) | collective-permute-done | bytes 294944 | tf_op jit(solution)/shard_map/ppermute | solution.py:18
  330.9 3.7 collective-permute-done.29
  335.1 4.1 %collective-permute-start.31 = (bf16[3,1,9,128,128]{4,3,2,1,0:T(8,128)(2,1)S(1)}, bf16[3,1,9,128,128]{4,3,2,1,0:T(8,128)(2,1)S(1)}, u32[]{:S(2)}, u32[]{:S(2)}) collective-permute-start(bf16[3,1,9,128,128]{4,3,2,1,0:T(8,128)(2,1)S(1)} %pad_maximum_fusion.6), channel_id=1, source_target_pairs={{1,0},{2,1},{3,2},{4,3},{5,4},{6,5},{7,6},{0,7},{9,8},{10,9},{11,1... | collective-permute-start | bytes 2654216 | tf_op jit(solution)/shard_map/ppermute | solution.py:21
  339.7 33.1 %collective-permute-done.30 = bf16[3,1,9,128,128]{4,3,2,1,0:T(8,128)(2,1)S(1)} collective-permute-done((bf16[3,1,9,128,128]{4,3,2,1,0:T(8,128)(2,1)S(1)}, bf16[3,1,9,128,128]{4,3,2,1,0:T(8,128)(2,1)S(1)}, u32[]{:S(2)}, u32[]{:S(2)}) %collective-permute-start.30) | collective-permute-done | bytes 884768 | tf_op jit(solution)/shard_map/ppermute | solution.py:18
  373.3 1.8 collective-permute-done.31
  (237 shorter events, 24.7 us)
Async XLA Ops:
  0.6 1.9 copy-start.1
  5.8 1.4 copy-start.3
  28.3 2.6 copy-start
  28.3 3.8 %slice-start = ((s8[5308416]{0:T(1024)(128)(4,1)}), s8[4194304]{0:T(1024)(128)(4,1)S(1)}, s32[]{:S(2)}) async-start(s8[5308416]{0:T(1024)(128)(4,1)} %bitcast.799), calls=%async_computation | async-start | bytes 8388608
  30.9 1.7 slice-start.1
  33.0 35.2 %collective-permute-start.5 = (f32[2,6,128,128]{3,2,0,1:T(8,128)S(1)}, f32[2,6,128,128]{3,2,0,1:T(8,128)S(1)}, u32[]{:S(2)}, u32[]{:S(2)}) collective-permute-start(f32[2,6,128,128]{3,2,0,1:T(8,128)S(1)} %get-tuple-element.78), channel_id=1, source_target_pairs={{0,1},{1,2},{2,3},{3,4},{4,5},{5,6},{6,7},{7,0},{8,9},{9,10},{10,1... | collective-permute-start | bytes 2359304 | tf_op jit(solution)/shard_map/ppermute | solution.py:9
  35.1 38.1 %collective-permute-start.6 = (f32[2,6,128,128]{3,2,0,1:T(8,128)S(1)}, f32[2,6,128,128]{3,2,0,1:T(8,128)S(1)}, u32[]{:S(2)}, u32[]{:S(2)}) collective-permute-start(f32[2,6,128,128]{3,2,0,1:T(8,128)S(1)} %get-tuple-element.76), channel_id=1, source_target_pairs={{0,7},{1,0},{2,1},{3,2},{4,3},{5,4},{6,5},{7,6},{8,15},{9,8},{10,9... | collective-permute-start | bytes 2359304 | tf_op jit(solution)/shard_map/ppermute | solution.py:9
  38.2 86.1 %collective-permute-start.2 = (f32[2,6,128,128]{3,2,0,1:T(8,128)S(1)}, f32[2,6,128,128]{3,2,0,1:T(8,128)S(1)}, u32[]{:S(2)}, u32[]{:S(2)}) collective-permute-start(f32[2,6,128,128]{3,2,0,1:T(8,128)S(1)} %get-tuple-element.79), channel_id=1, source_target_pairs={{0,8},{8,16},{16,24},{24,0},{1,9},{9,17},{17,25},{25,1},{2,10},{10... | collective-permute-start | bytes 2359304 | tf_op jit(solution)/shard_map/ppermute | solution.py:9
  40.5 29.3 %collective-permute-start.7 = (f32[2,4,128,128]{3,2,0,1:T(8,128)S(1)}, f32[2,4,128,128]{3,2,0,1:T(8,128)S(1)}, u32[]{:S(2)}, u32[]{:S(2)}) collective-permute-start(f32[2,4,128,128]{3,2,0,1:T(8,128)S(1)} %pad_maximum_fusion.9), channel_id=1, source_target_pairs={{0,24},{8,0},{16,8},{24,16},{1,25},{9,1},{17,9},{25,17},{2,26},{10... | collective-permute-start | bytes 1572872 | tf_op jit(solution)/shard_map/ppermute | solution.py:9
  40.7 30.3 %collective-permute-start.3 = (f32[2,4,128,128]{3,2,0,1:T(8,128)S(1)}, f32[2,4,128,128]{3,2,0,1:T(8,128)S(1)}, u32[]{:S(2)}, u32[]{:S(2)}) collective-permute-start(f32[2,4,128,128]{3,2,0,1:T(8,128)S(1)} %pad_maximum_fusion.8), channel_id=1, source_target_pairs={{0,8},{8,16},{16,24},{24,0},{1,9},{9,17},{17,25},{25,1},{2,10},{10... | collective-permute-start | bytes 1572872 | tf_op jit(solution)/shard_map/ppermute | solution.py:9
  42.5 0.7 copy-start.4
  68.1 15.3 %collective-permute-start.10 = (f32[2,4,128,128]{3,2,0,1:T(8,128)S(1)}, f32[2,4,128,128]{3,2,0,1:T(8,128)S(1)}, u32[]{:S(2)}, u32[]{:S(2)}) collective-permute-start(f32[2,4,128,128]{3,2,0,1:T(8,128)S(1)} %pad_maximum_fusion.10), channel_id=1, source_target_pairs={{0,24},{8,0},{16,8},{24,16},{1,25},{9,1},{17,9},{25,17},{2,26},{10... | collective-permute-start | bytes 1572872 | tf_op jit(solution)/shard_map/ppermute | solution.py:9
  69.8 13.6 %collective-permute-start = (f32[2,4,128,128]{3,2,0,1:T(8,128)S(1)}, f32[2,4,128,128]{3,2,0,1:T(8,128)S(1)}, u32[]{:S(2)}, u32[]{:S(2)}) collective-permute-start(f32[2,4,128,128]{3,2,0,1:T(8,128)S(1)} %pad_maximum_fusion.7), channel_id=1, source_target_pairs={{0,8},{8,16},{16,24},{24,0},{1,9},{9,17},{17,25},{25,1},{2,10},{10... | collective-permute-start | bytes 1572872 | tf_op jit(solution)/shard_map/ppermute | solution.py:9
  71.0 36.3 %collective-permute-start.8 = (f32[2,4,128,128]{3,2,0,1:T(8,128)S(1)}, f32[2,4,128,128]{3,2,0,1:T(8,128)S(1)}, u32[]{:S(2)}, u32[]{:S(2)}) collective-permute-start(f32[2,4,128,128]{3,2,0,1:T(8,128)S(1)} %collective-permute-done.7), channel_id=1, source_target_pairs={{0,1},{1,2},{2,3},{3,4},{4,5},{5,6},{6,7},{7,0},{8,9},{9,10},{10,1... | collective-permute-start | bytes 1572872 | tf_op jit(solution)/shard_map/ppermute | solution.py:9
  73.2 36.1 %collective-permute-start.4 = (f32[2,4,128,128]{3,2,0,1:T(8,128)S(1)}, f32[2,4,128,128]{3,2,0,1:T(8,128)S(1)}, u32[]{:S(2)}, u32[]{:S(2)}) collective-permute-start(f32[2,4,128,128]{3,2,0,1:T(8,128)S(1)} %collective-permute-done.3), channel_id=1, source_target_pairs={{0,7},{1,0},{2,1},{3,2},{4,3},{5,4},{6,5},{7,6},{8,15},{9,8},{10,9... | collective-permute-start | bytes 1572872 | tf_op jit(solution)/shard_map/ppermute | solution.py:9
  83.4 40.8 %collective-permute-start.9 = (f32[2,6,128,128]{3,2,0,1:T(8,128)S(1)}, f32[2,6,128,128]{3,2,0,1:T(8,128)S(1)}, u32[]{:S(2)}, u32[]{:S(2)}) collective-permute-start(f32[2,6,128,128]{3,2,0,1:T(8,128)S(1)} %get-tuple-element.75), channel_id=1, source_target_pairs={{0,24},{8,0},{16,8},{24,16},{1,25},{9,1},{17,9},{25,17},{2,26},{10... | collective-permute-start | bytes 2359304 | tf_op jit(solution)/shard_map/ppermute | solution.py:9
  83.4 26.1 %collective-permute-start.11 = (f32[2,4,128,128]{3,2,0,1:T(8,128)S(1)}, f32[2,4,128,128]{3,2,0,1:T(8,128)S(1)}, u32[]{:S(2)}, u32[]{:S(2)}) collective-permute-start(f32[2,4,128,128]{3,2,0,1:T(8,128)S(1)} %collective-permute-done.10), channel_id=1, source_target_pairs={{0,7},{1,0},{2,1},{3,2},{4,3},{5,4},{6,5},{7,6},{8,15},{9,8},{10,9... | collective-permute-start | bytes 1572872 | tf_op jit(solution)/shard_map/ppermute | solution.py:9
  107.2 16.9 %collective-permute-start.1 = (f32[2,4,128,128]{3,2,0,1:T(8,128)S(1)}, f32[2,4,128,128]{3,2,0,1:T(8,128)S(1)}, u32[]{:S(2)}, u32[]{:S(2)}) collective-permute-start(f32[2,4,128,128]{3,2,0,1:T(8,128)S(1)} %collective-permute-done), channel_id=1, source_target_pairs={{0,1},{1,2},{2,3},{3,4},{4,5},{5,6},{6,7},{7,0},{8,9},{9,10},{10,1... | collective-permute-start | bytes 1572872 | tf_op jit(solution)/shard_map/ppermute | solution.py:9
  125.3 2.2 copy-start.2
  126.6 5.5 %collective-permute-start.15 = (bf16[1,1,9,128,128]{4,3,2,1,0:T(8,128)(2,1)S(1)}, bf16[1,1,9,128,128]{4,3,2,1,0:T(8,128)(2,1)S(1)}, u32[]{:S(2)}, u32[]{:S(2)}) collective-permute-start(bf16[1,1,9,128,128]{4,3,2,1,0:T(8,128)(2,1)S(1)} %get-tuple-element.57), channel_id=1, source_target_pairs={{0,8},{8,16},{16,24},{24,0},{1,9},{9,17},{17,25},{25,1},{2,10},{10... | collective-permute-start | bytes 884744 | tf_op jit(solution)/shard_map/ppermute | solution.py:18
  127.4 9.6 %collective-permute-start.16 = (bf16[1,1,9,128,128]{4,3,2,1,0:T(8,128)(2,1)S(1)}, bf16[1,1,9,128,128]{4,3,2,1,0:T(8,128)(2,1)S(1)}, u32[]{:S(2)}, u32[]{:S(2)}) collective-permute-start(bf16[1,1,9,128,128]{4,3,2,1,0:T(8,128)(2,1)S(1)} %get-tuple-element.57), channel_id=1, source_target_pairs={{8,0},{16,8},{24,16},{0,24},{9,1},{17,9},{25,17},{1,25},{10,2},{18... | collective-permute-start | bytes 884744 | tf_op jit(solution)/shard_map/ppermute | solution.py:21
  127.9 10.5 %collective-permute-start.12 = (bf16[1,1,9,128,128]{3,4,2,1,0:T(8,128)(2,1)S(1)}, bf16[1,1,9,128,128]{3,4,2,1,0:T(8,128)(2,1)S(1)}, u32[]{:S(2)}, u32[]{:S(2)}) collective-permute-start(bf16[1,1,9,128,128]{3,4,2,1,0:T(8,128)(2,1)S(1)} %broadcast_multiply_fusion), channel_id=1, source_target_pairs={{0,8},{8,16},{16,24},{24,0},{1,9},{9,17},{17,25},{25,1},{2,10},{10... | collective-permute-start | bytes 884744 | tf_op jit(solution)/shard_map/ppermute | solution.py:18
  129.5 13.3 %collective-permute-start.13 = (bf16[1,1,9,128,128]{3,4,2,1,0:T(8,128)(2,1)S(1)}, bf16[1,1,9,128,128]{3,4,2,1,0:T(8,128)(2,1)S(1)}, u32[]{:S(2)}, u32[]{:S(2)}) collective-permute-start(bf16[1,1,9,128,128]{3,4,2,1,0:T(8,128)(2,1)S(1)} %broadcast_multiply_fusion), channel_id=1, source_target_pairs={{8,0},{16,8},{24,16},{0,24},{9,1},{17,9},{25,17},{1,25},{10,2},{18... | collective-permute-start | bytes 884744 | tf_op jit(solution)/shard_map/ppermute | solution.py:21
  137.1 57.4 %collective-permute-start.17 = (bf16[3,1,9,128,128]{4,3,2,1,0:T(8,128)(2,1)S(1)}, bf16[3,1,9,128,128]{4,3,2,1,0:T(8,128)(2,1)S(1)}, u32[]{:S(2)}, u32[]{:S(2)}) collective-permute-start(bf16[3,1,9,128,128]{4,3,2,1,0:T(8,128)(2,1)S(1)} %pad_maximum_fusion.3), channel_id=1, source_target_pairs={{0,1},{1,2},{2,3},{3,4},{4,5},{5,6},{6,7},{7,0},{8,9},{9,10},{10,1... | collective-permute-start | bytes 2654216 | tf_op jit(solution)/shard_map/ppermute | solution.py:18
  142.9 77.0 %collective-permute-start.14 = (bf16[3,1,9,128,128]{3,4,2,1,0:T(8,128)(2,1)S(1)}, bf16[3,1,9,128,128]{3,4,2,1,0:T(8,128)(2,1)S(1)}, u32[]{:S(2)}, u32[]{:S(2)}) collective-permute-start(bf16[3,1,9,128,128]{3,4,2,1,0:T(8,128)(2,1)S(1)} %pad_maximum_fusion.2), channel_id=1, source_target_pairs={{0,1},{1,2},{2,3},{3,4},{4,5},{5,6},{6,7},{7,0},{8,9},{9,10},{10,1... | collective-permute-start | bytes 2654216 | tf_op jit(solution)/shard_map/ppermute | solution.py:18
  143.0 77.7 %collective-permute-start.19 = (bf16[3,1,9,128,128]{3,4,2,1,0:T(8,128)(2,1)S(1)}, bf16[3,1,9,128,128]{3,4,2,1,0:T(8,128)(2,1)S(1)}, u32[]{:S(2)}, u32[]{:S(2)}) collective-permute-start(bf16[3,1,9,128,128]{3,4,2,1,0:T(8,128)(2,1)S(1)} %pad_maximum_fusion.2), channel_id=1, source_target_pairs={{1,0},{2,1},{3,2},{4,3},{5,4},{6,5},{7,6},{0,7},{9,8},{10,9},{11,1... | collective-permute-start | bytes 2654216 | tf_op jit(solution)/shard_map/ppermute | solution.py:21
  147.4 70.9 %collective-permute-start.18 = (bf16[3,1,9,128,128]{4,3,2,1,0:T(8,128)(2,1)S(1)}, bf16[3,1,9,128,128]{4,3,2,1,0:T(8,128)(2,1)S(1)}, u32[]{:S(2)}, u32[]{:S(2)}) collective-permute-start(bf16[3,1,9,128,128]{4,3,2,1,0:T(8,128)(2,1)S(1)} %pad_maximum_fusion.3), channel_id=1, source_target_pairs={{1,0},{2,1},{3,2},{4,3},{5,4},{6,5},{7,6},{0,7},{9,8},{10,9},{11,1... | collective-permute-start | bytes 2654216 | tf_op jit(solution)/shard_map/ppermute | solution.py:21
  222.2 5.4 %collective-permute-start.20 = (bf16[1,1,9,128,128]{4,3,2,1,0:T(8,128)(2,1)S(1)}, bf16[1,1,9,128,128]{4,3,2,1,0:T(8,128)(2,1)S(1)}, u32[]{:S(2)}, u32[]{:S(2)}) collective-permute-start(bf16[1,1,9,128,128]{4,3,2,1,0:T(8,128)(2,1)S(1)} %multiply_convert_fusion.7), channel_id=1, source_target_pairs={{0,8},{8,16},{16,24},{24,0},{1,9},{9,17},{17,25},{25,1},{2,10},{10... | collective-permute-start | bytes 884744 | tf_op jit(solution)/shard_map/ppermute | solution.py:18
  222.7 8.6 %collective-permute-start.21 = (bf16[1,1,9,128,128]{4,3,2,1,0:T(8,128)(2,1)S(1)}, bf16[1,1,9,128,128]{4,3,2,1,0:T(8,128)(2,1)S(1)}, u32[]{:S(2)}, u32[]{:S(2)}) collective-permute-start(bf16[1,1,9,128,128]{4,3,2,1,0:T(8,128)(2,1)S(1)} %multiply_convert_fusion.7), channel_id=1, source_target_pairs={{8,0},{16,8},{24,16},{0,24},{9,1},{17,9},{25,17},{1,25},{10,2},{18... | collective-permute-start | bytes 884744 | tf_op jit(solution)/shard_map/ppermute | solution.py:21
  231.4 38.3 %collective-permute-start.22 = (bf16[3,1,9,128,128]{4,3,2,1,0:T(8,128)(2,1)S(1)}, bf16[3,1,9,128,128]{4,3,2,1,0:T(8,128)(2,1)S(1)}, u32[]{:S(2)}, u32[]{:S(2)}) collective-permute-start(bf16[3,1,9,128,128]{4,3,2,1,0:T(8,128)(2,1)S(1)} %pad_maximum_fusion.4), channel_id=1, source_target_pairs={{0,1},{1,2},{2,3},{3,4},{4,5},{5,6},{6,7},{7,0},{8,9},{9,10},{10,1... | collective-permute-start | bytes 2654216 | tf_op jit(solution)/shard_map/ppermute | solution.py:18
  231.8 40.2 %collective-permute-start.23 = (bf16[3,1,9,128,128]{4,3,2,1,0:T(8,128)(2,1)S(1)}, bf16[3,1,9,128,128]{4,3,2,1,0:T(8,128)(2,1)S(1)}, u32[]{:S(2)}, u32[]{:S(2)}) collective-permute-start(bf16[3,1,9,128,128]{4,3,2,1,0:T(8,128)(2,1)S(1)} %pad_maximum_fusion.4), channel_id=1, source_target_pairs={{1,0},{2,1},{3,2},{4,3},{5,4},{6,5},{7,6},{0,7},{9,8},{10,9},{11,1... | collective-permute-start | bytes 2654216 | tf_op jit(solution)/shard_map/ppermute | solution.py:21
  273.4 5.8 %collective-permute-start.24 = (bf16[1,1,9,128,128]{4,3,2,1,0:T(8,128)(2,1)S(1)}, bf16[1,1,9,128,128]{4,3,2,1,0:T(8,128)(2,1)S(1)}, u32[]{:S(2)}, u32[]{:S(2)}) collective-permute-start(bf16[1,1,9,128,128]{4,3,2,1,0:T(8,128)(2,1)S(1)} %subtract_convert_fusion.1), channel_id=1, source_target_pairs={{0,8},{8,16},{16,24},{24,0},{1,9},{9,17},{17,25},{25,1},{2,10},{10... | collective-permute-start | bytes 884744 | tf_op jit(solution)/shard_map/ppermute | solution.py:18
  274.3 8.6 %collective-permute-start.25 = (bf16[1,1,9,128,128]{4,3,2,1,0:T(8,128)(2,1)S(1)}, bf16[1,1,9,128,128]{4,3,2,1,0:T(8,128)(2,1)S(1)}, u32[]{:S(2)}, u32[]{:S(2)}) collective-permute-start(bf16[1,1,9,128,128]{4,3,2,1,0:T(8,128)(2,1)S(1)} %subtract_convert_fusion.1), channel_id=1, source_target_pairs={{8,0},{16,8},{24,16},{0,24},{9,1},{17,9},{25,17},{1,25},{10,2},{18... | collective-permute-start | bytes 884744 | tf_op jit(solution)/shard_map/ppermute | solution.py:21
  283.0 38.1 %collective-permute-start.26 = (bf16[3,1,9,128,128]{4,3,2,1,0:T(8,128)(2,1)S(1)}, bf16[3,1,9,128,128]{4,3,2,1,0:T(8,128)(2,1)S(1)}, u32[]{:S(2)}, u32[]{:S(2)}) collective-permute-start(bf16[3,1,9,128,128]{4,3,2,1,0:T(8,128)(2,1)S(1)} %pad_maximum_fusion.5), channel_id=1, source_target_pairs={{0,1},{1,2},{2,3},{3,4},{4,5},{5,6},{6,7},{7,0},{8,9},{9,10},{10,1... | collective-permute-start | bytes 2654216 | tf_op jit(solution)/shard_map/ppermute | solution.py:18
  283.5 39.9 %collective-permute-start.27 = (bf16[3,1,9,128,128]{4,3,2,1,0:T(8,128)(2,1)S(1)}, bf16[3,1,9,128,128]{4,3,2,1,0:T(8,128)(2,1)S(1)}, u32[]{:S(2)}, u32[]{:S(2)}) collective-permute-start(bf16[3,1,9,128,128]{4,3,2,1,0:T(8,128)(2,1)S(1)} %pad_maximum_fusion.5), channel_id=1, source_target_pairs={{1,0},{2,1},{3,2},{4,3},{5,4},{6,5},{7,6},{0,7},{9,8},{10,9},{11,1... | collective-permute-start | bytes 2654216 | tf_op jit(solution)/shard_map/ppermute | solution.py:21
  324.8 6.1 %collective-permute-start.28 = (bf16[1,1,9,128,128]{4,3,2,1,0:T(8,128)(2,1)S(1)}, bf16[1,1,9,128,128]{4,3,2,1,0:T(8,128)(2,1)S(1)}, u32[]{:S(2)}, u32[]{:S(2)}) collective-permute-start(bf16[1,1,9,128,128]{4,3,2,1,0:T(8,128)(2,1)S(1)} %multiply_convert_fusion.5), channel_id=1, source_target_pairs={{0,8},{8,16},{16,24},{24,0},{1,9},{9,17},{17,25},{25,1},{2,10},{10... | collective-permute-start | bytes 884744 | tf_op jit(solution)/shard_map/ppermute | solution.py:18
  326.0 8.6 %collective-permute-start.29 = (bf16[1,1,9,128,128]{4,3,2,1,0:T(8,128)(2,1)S(1)}, bf16[1,1,9,128,128]{4,3,2,1,0:T(8,128)(2,1)S(1)}, u32[]{:S(2)}, u32[]{:S(2)}) collective-permute-start(bf16[1,1,9,128,128]{4,3,2,1,0:T(8,128)(2,1)S(1)} %multiply_convert_fusion.5), channel_id=1, source_target_pairs={{8,0},{16,8},{24,16},{0,24},{9,1},{17,9},{25,17},{1,25},{10,2},{18... | collective-permute-start | bytes 884744 | tf_op jit(solution)/shard_map/ppermute | solution.py:21
  334.7 38.1 %collective-permute-start.30 = (bf16[3,1,9,128,128]{4,3,2,1,0:T(8,128)(2,1)S(1)}, bf16[3,1,9,128,128]{4,3,2,1,0:T(8,128)(2,1)S(1)}, u32[]{:S(2)}, u32[]{:S(2)}) collective-permute-start(bf16[3,1,9,128,128]{4,3,2,1,0:T(8,128)(2,1)S(1)} %pad_maximum_fusion.6), channel_id=1, source_target_pairs={{0,1},{1,2},{2,3},{3,4},{4,5},{5,6},{6,7},{7,0},{8,9},{9,10},{10,1... | collective-permute-start | bytes 2654216 | tf_op jit(solution)/shard_map/ppermute | solution.py:18
  335.1 39.9 %collective-permute-start.31 = (bf16[3,1,9,128,128]{4,3,2,1,0:T(8,128)(2,1)S(1)}, bf16[3,1,9,128,128]{4,3,2,1,0:T(8,128)(2,1)S(1)}, u32[]{:S(2)}, u32[]{:S(2)}) collective-permute-start(bf16[3,1,9,128,128]{4,3,2,1,0:T(8,128)(2,1)S(1)} %pad_maximum_fusion.6), channel_id=1, source_target_pairs={{1,0},{2,1},{3,2},{4,3},{5,4},{6,5},{7,6},{0,7},{9,8},{10,9},{11,1... | collective-permute-start | bytes 2654216 | tf_op jit(solution)/shard_map/ppermute | solution.py:21
where the time goes:
time: 379 us; the launch traced here: 377 us
  waiting for transfers between devices  275 us (73%)
  starting transfers between devices  47.4 us (13%)
  local copies, waits for them, and re-layouts  23.4 us (6%)
  matrix products  19.9 us (5%)
  other arithmetic  9.1 us (2%)
    ppermute x10, waiting for transfers between devices, extended(): lax.ppermute(lax.slice_in_dim(block, block.shape[dim] - width, None, axis...  161 us
    ppermute x12, waiting for transfers between devices, from_behind(): lax.ppermute(value, axis, [(i, (i + by) % count) for i in range(count)])  65.3 us
    ppermute x10, waiting for transfers between devices, extended(): lax.ppermute(lax.slice_in_dim(block, 0, width, axis=dim), axis, backward)  49.3 us
    ppermute x12, starting transfers between devices, from_behind(): lax.ppermute(value, axis, [(i, (i + by) % count) for i in range(count)])  24.5 us
    ppermute x10, starting transfers between devices, extended(): lax.ppermute(lax.slice_in_dim(block, 0, width, axis=dim), axis, backward)  17.5 us
    another operation x2, local copies, waits for them, and re-layouts, body(): blocks = jnp.stack([h_all, s_all]).reshape(2, 9, width, 9, width)  16.6 us
    dot_general x54, matrix products, block_product(): jnp.einsum('ij,pjk->pik', left[first], near[1 + fa, 1 + fb], preferred_el...  12.3 us
  transfers between devices with their start and end apart: 32, of which 22 were waited for; matrix products, arithmetic and copies ran while one was open for 3% of the time, Pallas kernels for 0%

commit v1 on v0

v1 whole, which is shorter than its diff:
```python
import functools

import jax
import jax.numpy as jnp
from jax import lax
from jax.experimental import pallas as pl
from jax.experimental.pallas import tpu as pltpu
from jax.sharding import PartitionSpec as P

MESH = pl.DeviceIdType.MESH
SPAN = (-1, 0, 1)


def part(d):
    return pl.ds(1, 2) if d == 1 else pl.ds(0, 2) if d == -1 else pl.ds(0, 3)


class Halo:
    def __init__(self, where, own, near, send, recv, sign=1, whole=False):
        self.where, self.own, self.near = where, own, near
        self.send, self.recv, self.sign, self.whole = send, recv, sign, whole
        self.direct = {}
        self.passed = {}

    def make(self, src, a, b, da, db, ta, tb, at):
        dst = self.near.at[a, b]
        if not self.whole:
            src = src.at[part(self.sign * da), part(self.sign * db)]
            dst = dst.at[part(self.sign * da), part(self.sign * db)]
        return pltpu.make_async_remote_copy(
            src_ref=src, dst_ref=dst, send_sem=self.send.at[at], recv_sem=self.recv.at[at],
            device_id=self.where(ta, tb), device_id_type=MESH,
        )

    def start(self):
        for at, (da, db) in enumerate(((0, 1), (0, -1), (1, 0), (-1, 0))):
            self.direct[da, db] = self.make(self.own, 1 - da, 1 - db, da, db, da, db, at)
            self.direct[da, db].start()

    def relay(self):
        at = 4
        for db in (1, -1):
            self.direct[0, db].wait_recv()
            for da in (1, -1):
                src = self.near.at[1, 1 - db]
                self.passed[da, db] = self.make(src, 1 - da, 1 - db, da, db, da, 0, at)
                self.passed[da, db].start()
                at += 1

    def finish(self):
        for da in (1, -1):
            self.direct[da, 0].wait_recv()
        for copy in self.passed.values():
            copy.wait_recv()

    def drain(self):
        for copy in list(self.direct.values()) + list(self.passed.values()):
            copy.wait_send()


def product(left, own, near, keep, emit):
    width = left.shape[-1]
    blank = jnp.zeros((width, width), jnp.bfloat16)
    for pa in SPAN:
        total = None
        for fa in SPAN:
            if abs(pa - fa) > 1:
                continue
            lhs = jnp.concatenate([left[fa + 1, fb + 1] for fb in SPAN], axis=1)
            rows = []
            for fb in SPAN:
                src = own if (fa, fb) == (0, 0) else near.at[fa + 1, fb + 1]
                rows.append(jnp.concatenate(
                    [src[pa - fa + 1, pb - fb + 1] if abs(pb - fb) <= 1 else blank for pb in SPAN],
                    axis=1,
                ))
            rhs = jnp.concatenate(rows, axis=0)
            term = jnp.dot(lhs, rhs, preferred_element_type=jnp.float32)
            total = term if total is None else total + term
        for pb in SPAN:
            cut = total[:, (pb + 1) * width:(pb + 2) * width]
            emit(pa + 1, pb + 1, cut * keep[pa + 1, pb + 1])


def overlap(lefts, rights, width, keep, emit):
    for pa in SPAN:
        total = None
        for ka in SPAN:
            if abs(ka - pa) > 1:
                continue
            for kb in SPAN:
                lhs = lefts(ka, kb)
                rhs = rights(ka, kb)
                blank = jnp.zeros(lhs.shape, jnp.bfloat16)
                rows = jnp.concatenate(
                    [rhs[ka - pa + 1, kb - pb + 1] if abs(kb - pb) <= 1 else blank for pb in SPAN],
                    axis=0,
                )
                term = lax.dot_general(
                    lhs, rows, (((1,), (1,)), ((), ())), preferred_element_type=jnp.float32
                )
                total = term if total is None else total + term
        for pb in SPAN:
            cut = total[:, (pb + 1) * width:(pb + 2) * width]
            emit(pa + 1, pb + 1, cut * keep[pa + 1, pb + 1])


def kernel(counts, orb, pot, den, keep, ham, mar, pur,
           o_near, v_near, w_near, d0_near, d1_near, m_near, t0_near, t1_near, first, send, recv):
    width, cells = orb.shape[-2], orb.shape[-1]
    me = (lax.axis_index("gx"), lax.axis_index("yz"))

    def where(da, db):
        return (
            lax.rem(me[0] + da + counts[0], counts[0]),
            lax.rem(me[1] + db + counts[1], counts[1]),
        )

    barrier = pltpu.get_barrier_semaphore()
    for da, db in ((0, 1), (0, -1), (1, 0), (-1, 0)):
        pl.semaphore_signal(barrier, inc=1, device_id=where(da, db), device_id_type=MESH)
    pl.semaphore_wait(barrier, 4)

    used = iter(range(7))

    def halo(own, near, **more):
        at = next(used)
        return Halo(where, own, near, send.at[at], recv.at[at], **more)

    waves = halo(orb, o_near, sign=-1)
    fields = halo(pot, v_near, whole=True)
    waves.start()
    fields.start()
    d_own = d0_near.at[1, 1]
    for a in range(3):
        for b in range(3):
            d_own[a, b] = (den[a, b].astype(jnp.float32) * keep[a, b]).astype(jnp.bfloat16)
    waves.relay()
    fields.relay()
    density = halo(d_own, d0_near)
    density.start()
    waves.finish()

    def region(ka, kb):
        return orb if (ka, kb) == (0, 0) else o_near.at[ka + 1, kb + 1]

    m_own = m_near.at[1, 1]

    def put_margin(a, b, value):
        mar[a, b] = value
        m_own[a, b] = value.astype(jnp.bfloat16)

    overlap(lambda ka, kb: region(ka, kb)[ka + 1, kb + 1], region, width, keep, put_margin)
    margin = halo(m_own, m_near)
    margin.start()
    density.relay()
    fields.finish()

    lane = lax.broadcasted_iota(jnp.int32, (width, 128), 1)
    for ka in SPAN:
        for kb in SPAN:
            src = region(ka, kb)
            field = pot[0] if (ka, kb) == (0, 0) else v_near[ka + 1, kb + 1, 0]
            for la in SPAN:
                for lb in SPAN:
                    if abs(ka - la) > 1 or abs(kb - lb) > 1:
                        continue
                    value = src[la + 1, lb + 1].astype(jnp.float32)
                    dst = w_near.at[ka + 1, kb + 1, la + 1, lb + 1]
                    dst[:, :cells] = (value * field).astype(jnp.bfloat16)
                    for line in range(cells // 128):
                        piece = value[:, line * 128:(line + 1) * 128]
                        ahead = pltpu.roll(piece, 127, 1)
                        step = jnp.where(lane < 127, ahead - piece, 0.0)
                        at = cells + line * 128
                        dst[:, at:at + 128] = step.astype(jnp.bfloat16)
    margin.relay()

    def h_left(ka, kb):
        half = w_near[ka + 1, kb + 1, ka + 1, kb + 1][:, cells:] * 0.5
        return jnp.concatenate([region(ka, kb)[ka + 1, kb + 1], half.astype(jnp.bfloat16)], axis=1)

    def put_ham(a, b, value):
        ham[a, b] = value

    overlap(h_left, lambda ka, kb: w_near.at[ka + 1, kb + 1], width, keep, put_ham)
    margin.finish()
    density.finish()

    def put_first(a, b, value):
        first[a, b] = value.astype(jnp.bfloat16)

    started = [waves, fields, density, margin]
    nears = ((d0_near, t0_near), (d1_near, t1_near))
    for turn, (d_near, t_near) in enumerate(nears):
        d_row, t_row = d_near.at[1, 1], t_near.at[1, 1]
        product(d_row, m_own, m_near, keep, put_first)
        if turn:
            rows.relay()
            rows.finish()

        def put_third(a, b, value):
            pur[a, b] = 3.0 * value
            t_row[a, b] = value.astype(jnp.bfloat16)

        product(first, d_row, d_near, keep, put_third)
        cubic = halo(t_row, t_near)
        cubic.start()
        cubic.relay()
        cubic.finish()
        started.append(cubic)
        after = nears[turn + 1][0].at[1, 1] if turn + 1 < len(nears) else None

        def put_fifth(a, b, value):
            result = pur[a, b] - 2.0 * value
            pur[a, b] = result
            if after is not None:
                after[a, b] = result.astype(jnp.bfloat16)

        product(first, t_row, t_near, keep, put_fifth)
        if after is not None:
            rows = halo(after, nears[turn + 1][0])
            rows.start()
            started.append(rows)
    for one in started:
        one.drain()


def body(counts, orbitals, potential, density, pattern):
    width, cells = orbitals.shape[3], orbitals.shape[4]
    keep = jnp.broadcast_to(
        pattern.reshape(3, 3, 1, 1).astype(jnp.float32), (3, 3, 1, 128)
    )
    near = pltpu.VMEM((3, 3, 3, 3, width, width), jnp.bfloat16)
    blocks = jax.ShapeDtypeStruct((3, 3, width, width), jnp.float32)
    vmem = pl.BlockSpec(memory_space=pltpu.VMEM)
    outs = pl.pallas_call(
        functools.partial(kernel, counts),
        out_shape=(blocks,) * 3,
        in_specs=[vmem] * 4,
        out_specs=(vmem,) * 3,
        scratch_shapes=[
            pltpu.VMEM((3, 3, 3, 3, width, cells), jnp.bfloat16),
            pltpu.VMEM((3, 3, 1, 1, cells), jnp.float32),
            pltpu.VMEM((3, 3, 3, 3, width, 2 * cells), jnp.bfloat16),
            near, near, near, near, near,
            pltpu.VMEM((3, 3, width, width), jnp.bfloat16),
            pltpu.SemaphoreType.DMA((7, 8)),
            pltpu.SemaphoreType.DMA((7, 8)),
        ],
        compiler_params=pltpu.CompilerParams(
            collective_id=0, has_side_effects=True, vmem_limit_bytes=60 * 2**20
        ),
    )(
        orbitals.reshape(3, 3, width, cells),
        potential.reshape(1, 1, cells),
        density.reshape(3, 3, width, width),
        keep,
    )
    return tuple(out.reshape(1, 1, 9, width, width) for out in outs)


def solution(mesh):
    rows = P("gx", "yz", None, None, None)
    flat = P("gx", "yz", None)
    return jax.shard_map(
        functools.partial(body, (mesh.shape["gx"], mesh.shape["yz"])),
        mesh=mesh,
        in_specs=(rows, flat, rows, flat),
        out_specs=(rows,) * 3,
        check_vma=False,
    )
```

time: 379 us -> 116 us (0.31)
  waiting for transfers between devices: 275 us -> 0 us
  Pallas kernels: 0 us -> 110 us
  starting transfers between devices: 47.4 us -> 0 us
  matrix products: 19.9 us -> 0 us
  local copies, waits for them, and re-layouts: 23.4 us -> 5.48 us
  other arithmetic: 9.1 us -> 0.02 us
    ppermute x32 -> x0, waiting for transfers between devices: 275 us -> none  [the longest x10 161 us: extended(): lax.ppermute(lax.slice_in_dim(block, block.shape[dim] - width, None, axis...]
    pallas_call x0 -> x1, Pallas kernels: none -> 110 us  [body(): pl.pallas_call(functools.partial(kernel, counts), out_shape=(blocks,) * 3...]
    ppermute x32 -> x0, starting transfers between devices: 47.4 us -> none  [the longest x12 24.5 us: from_behind(): lax.ppermute(value, axis, [(i, (i + by) % count) for i in range(count)])]
    dot_general x57 -> x0, matrix products: 19.9 us -> none  [the longest x54 12.3 us: block_product(): jnp.einsum('ij,pjk->pik', left[first], near[1 + fa, 1 + fb], preferred_el...]
    another operation x12 -> x0, local copies, waits for them, and re-layouts: 16.7 us -> none  [the longest x2 16.6 us: body(): blocks = jnp.stack([h_all, s_all]).reshape(2, 9, width, 9, width)]
  transfers between devices with their start and end apart: 32 -> 0, of which waited for: 22 -> 0; matrix products, arithmetic and copies ran while one was open for 3% -> 0% of each run, Pallas kernels for 0% -> 0%
where the time goes in v1:
time: 116 us
  Pallas kernels  110 us (95%)
  local copies, waits for them, and re-layouts  5.48 us (5%)
    pallas_call x1, Pallas kernels, body(): pl.pallas_call(functools.partial(kernel, counts), out_shape=(blocks,) * 3...  110 us
    unnamed x9, local copies, waits for them, and re-layouts  4.72 us

profile of v1, /device:TPU:1, one launch (start us, length us, event | category | flops | bytes accessed | tf_op | source)
XLA Modules:
  0.0 115.8 jit_solution(3692681839949769090)
XLA Ops:
  0.6 0.0 copy-start.2
  0.6 0.6 copy-done.2
  1.3 0.1 convert_element_type.12
  1.4 0.7 broadcast_in_dim.2.keep
  2.1 109.7 %shard_map.67 = (f32[3,3,128,128]{3,2,1,0:T(8,128)}, f32[3,3,128,128]{3,2,1,0:T(8,128)}, f32[3,3,128,128]{3,2,1,0:T(8,128)}) custom-call(bf16[3,3,128,256]{3,2,1,0:T(8,128)(2,1)} %bitcast.8, f32[1,1,256]{2,1,0:T(1,128)} %pot.1, bf16[3,3,128,128]{3,2,1,0:T(8,128)(2,1)} %bitcast.9, f32[3,3,1,128]{3,2,1,0:T(1,128)} %broadcast_in_dim.2.keep), custom_call_target="tpu_custom_call" | custom-call | tf_op jit(solution)/shard_map/pallas_call | solution.py:237
  111.7 0.0 copy-start.1
  111.7 2.0 %copy.10 = f32[1,1,9,128,128]{4,3,2,1,0:T(8,128)} copy(f32[1,1,9,128,128]{4,3,2,1,0:T(8,128)} %bitcast.7) | data formatting | bytes 1179648
  113.7 0.0 copy-done.1
  113.7 0.0 copy-start
  113.7 0.8 copy.11
  114.5 0.5 copy-done
  115.0 0.8 copy.12
  (1 shorter events, 0.0 us)
Async XLA Ops:
  0.6 0.7 copy-start.2
  111.7 2.0 %copy-start.1 = (f32[3,3,128,128]{3,2,1,0:T(8,128)S(1)}, f32[3,3,128,128]{3,2,1,0:T(8,128)}, u32[]{:S(2)}) copy-start(f32[3,3,128,128]{3,2,1,0:T(8,128)} %get-tuple-element.7) | copy-start | bytes 1769476
  113.7 1.3 %copy-start = (f32[3,3,128,128]{3,2,1,0:T(8,128)S(1)}, f32[3,3,128,128]{3,2,1,0:T(8,128)}, u32[]{:S(2)}) copy-start(f32[3,3,128,128]{3,2,1,0:T(8,128)} %get-tuple-element.8) | copy-start | bytes 1769476

commit v2 on v1

--- a/solution.py
+++ b/solution.py
@@ -16,45 +16,74 @@
 
 
 class Halo:
-    def __init__(self, where, own, near, send, recv, sign=1, whole=False):
+    def __init__(self, where, own, near, send, recv, sign=1, whole=False, slim=False):
         self.where, self.own, self.near = where, own, near
-        self.send, self.recv, self.sign, self.whole = send, recv, sign, whole
+        self.send, self.recv, self.sign, self.whole, self.slim = send, recv, sign, whole, slim
+        outer = 2 * lax.rem(lax.axis_index("gx"), 2) - 1
+        self.order = [
+            (db, piece, pa, das)
+            for piece, pa, das in (
+                ((0, None, (1, -1)),) if whole else
+                ((0, 1, (1, -1)), (1, 0, ()), (2, 2, ())) if slim else (
+                    (0, 1, (outer, -outer)),
+                    (1, 1 + sign * outer, (outer,)),
+                    (2, 1 - sign * outer, (-outer,)),
+                )
+            )
+            for db in (1, -1)
+        ]
         self.direct = {}
-        self.passed = {}
-
-    def make(self, src, a, b, da, db, ta, tb, at):
-        dst = self.near.at[a, b]
+        self.passed = []
+        self.next = 0
+
+    def make(self, src, da, db, ta, tb, pa, pb=None):
+        dst = self.near.at[1 - da, 1 - db]
         if not self.whole:
-            src = src.at[part(self.sign * da), part(self.sign * db)]
-            dst = dst.at[part(self.sign * da), part(self.sign * db)]
-        return pltpu.make_async_remote_copy(
+            pb = part(self.sign * db) if pb is None else pb
+            src = src.at[pa, pb]
+            dst = dst.at[pa, pb]
+        at = self.next
+        self.next += 1
+        copy = pltpu.make_async_remote_copy(
             src_ref=src, dst_ref=dst, send_sem=self.send.at[at], recv_sem=self.recv.at[at],
             device_id=self.where(ta, tb), device_id_type=MESH,
         )
+        copy.start()
+        return copy
+
+    def start_far(self):
+        for db, piece, pa, _ in self.order:
+            self.direct[db, piece] = self.make(self.own, 0, db, 0, db, pa)
+
+    def start_near(self):
+        for da in (1, -1):
+            pa = 1 if self.slim else part(self.sign * da)
+            self.direct[da] = self.make(self.own, da, 0, da, 0, pa)
 
     def start(self):
-        for at, (da, db) in enumerate(((0, 1), (0, -1), (1, 0), (-1, 0))):
-            self.direct[da, db] = self.make(self.own, 1 - da, 1 - db, da, db, da, db, at)
-            self.direct[da, db].start()
+        self.start_far()
+        self.start_near()
 
     def relay(self):
-        at = 4
-        for db in (1, -1):
-            self.direct[0, db].wait_recv()
-            for da in (1, -1):
+        for db, piece, pa, das in self.order:
+            if das:
+                self.direct[db, piece].wait_recv()
+            for da in das:
                 src = self.near.at[1, 1 - db]
-                self.passed[da, db] = self.make(src, 1 - da, 1 - db, da, db, da, 0, at)
-                self.passed[da, db].start()
-                at += 1
+                pb = 1 if self.slim else None
+                self.passed.append(self.make(src, da, db, da, 0, pa, pb))
 
     def finish(self):
+        for db, piece, _, das in self.order:
+            if not das:
+                self.direct[db, piece].wait_recv()
         for da in (1, -1):
-            self.direct[da, 0].wait_recv()
-        for copy in self.passed.values():
+            self.direct[da].wait_recv()
+        for copy in self.passed:
             copy.wait_recv()
 
     def drain(self):
-        for copy in list(self.direct.values()) + list(self.passed.values()):
+        for copy in list(self.direct.values()) + self.passed:
             copy.wait_send()
 
 
@@ -82,7 +111,7 @@
             emit(pa + 1, pb + 1, cut * keep[pa + 1, pb + 1])
 
 
-def overlap(lefts, rights, width, keep, emit):
+def overlap(lefts, rights, width, emit):
     for pa in SPAN:
         total = None
         for ka in SPAN:
@@ -102,11 +131,11 @@
                 total = term if total is None else total + term
         for pb in SPAN:
             cut = total[:, (pb + 1) * width:(pb + 2) * width]
-            emit(pa + 1, pb + 1, cut * keep[pa + 1, pb + 1])
-
-
-def kernel(counts, orb, pot, den, keep, ham, mar, pur,
-           o_near, v_near, w_near, d0_near, d1_near, m_near, t0_near, t1_near, first, send, recv):
+            emit(pa + 1, pb + 1, cut)
+
+
+def kernel(counts, orb, pot, den, pattern, ham, mar, pur,
+           o_near, v_near, w_near, d0_near, d1_near, m_near, u_near, t0_near, t1_near, first, send, recv):
     width, cells = orb.shape[-2], orb.shape[-1]
     me = (lax.axis_index("gx"), lax.axis_index("yz"))
 
@@ -116,6 +145,9 @@
             lax.rem(me[1] + db + counts[1], counts[1]),
         )
 
+    keep = {
+        (a, b): pattern[3 * a + b].astype(jnp.float32) for a in range(3) for b in range(3)
+    }
     barrier = pltpu.get_barrier_semaphore()
     for da, db in ((0, 1), (0, -1), (1, 0), (-1, 0)):
         pl.semaphore_signal(barrier, inc=1, device_id=where(da, db), device_id_type=MESH)
@@ -128,39 +160,29 @@
         return Halo(where, own, near, send.at[at], recv.at[at], **more)
 
     waves = halo(orb, o_near, sign=-1)
-    fields = halo(pot, v_near, whole=True)
+    v_own = v_near.at[1, 1]
+    v_own[0:1] = pot[0]
+    for a in range(3):
+        for b in range(3):
+            at = 1 + 3 * a + b
+            v_own[at:at + 1] = jnp.full((1, cells), keep[a, b], jnp.float32)
+    fields = halo(v_own, v_near, whole=True)
+    fields.start()
     waves.start()
-    fields.start()
     d_own = d0_near.at[1, 1]
     for a in range(3):
         for b in range(3):
             d_own[a, b] = (den[a, b].astype(jnp.float32) * keep[a, b]).astype(jnp.bfloat16)
-    waves.relay()
-    fields.relay()
     density = halo(d_own, d0_near)
-    density.start()
-    waves.finish()
-
+    density.start_far()
     def region(ka, kb):
         return orb if (ka, kb) == (0, 0) else o_near.at[ka + 1, kb + 1]
 
-    m_own = m_near.at[1, 1]
-
-    def put_margin(a, b, value):
-        mar[a, b] = value
-        m_own[a, b] = value.astype(jnp.bfloat16)
-
-    overlap(lambda ka, kb: region(ka, kb)[ka + 1, kb + 1], region, width, keep, put_margin)
-    margin = halo(m_own, m_near)
-    margin.start()
-    density.relay()
-    fields.finish()
-
-    lane = lax.broadcasted_iota(jnp.int32, (width, 128), 1)
-    for ka in SPAN:
-        for kb in SPAN:
+    def prepare(regions):
+        lane = lax.broadcasted_iota(jnp.int32, (width, 128), 1)
+        for ka, kb in regions:
             src = region(ka, kb)
-            field = pot[0] if (ka, kb) == (0, 0) else v_near[ka + 1, kb + 1, 0]
+            field = pot[0] if (ka, kb) == (0, 0) else v_near[ka + 1, kb + 1, 0:1]
             for la in SPAN:
                 for lb in SPAN:
                     if abs(ka - la) > 1 or abs(kb - lb) > 1:
@@ -174,6 +196,27 @@
                         step = jnp.where(lane < 127, ahead - piece, 0.0)
                         at = cells + line * 128
                         dst[:, at:at + 128] = step.astype(jnp.bfloat16)
+
+    fields.relay()
+    prepare([(0, 0)])
+    waves.relay()
+    density.start_near()
+    prepare([(0, 1), (0, -1)])
+    waves.finish()
+
+    m_own, u_own = m_near.at[1, 1], u_near.at[1, 1]
+
+    def put_margin(a, b, value):
+        kept = value * keep[a, b]
+        mar[a, b] = kept
+        m_own[a, b] = kept.astype(jnp.bfloat16)
+        u_own[a, b] = value.astype(jnp.bfloat16)
+
+    overlap(lambda ka, kb: region(ka, kb)[ka + 1, kb + 1], region, width, put_margin)
+    margin = halo(u_own, u_near, slim=True)
+    margin.start()
+    fields.finish()
+    density.relay()
     margin.relay()
 
     def h_left(ka, kb):
@@ -181,10 +224,30 @@
         return jnp.concatenate([region(ka, kb)[ka + 1, kb + 1], half.astype(jnp.bfloat16)], axis=1)
 
     def put_ham(a, b, value):
-        ham[a, b] = value
-
-    overlap(h_left, lambda ka, kb: w_near.at[ka + 1, kb + 1], width, keep, put_ham)
+        ham[a, b] = value * keep[a, b]
+
+    def complete(local):
+        for ja in SPAN:
+            for jb in SPAN:
+                for ka in SPAN:
+                    for kb in SPAN:
+                        pa, pb = ka - ja, kb - jb
+                        if (ja, jb) == (0, 0) or abs(pa) > 1 or abs(pb) > 1:
+                            continue
+                        if local != ((ka, kb) == (0, 0)):
+                            continue
+                        sent = (pa, pb) == (0, 0) or ja == 0 or (jb == 0 and pa == 0)
+                        if sent and not local:
+                            block = u_near[ja + 1, jb + 1, pa + 1, pb + 1].astype(jnp.float32)
+                        else:
+                            block = u_near[ka + 1, kb + 1, 1 - pa, 1 - pb].astype(jnp.float32).T
+                        at = 1 + 3 * (pa + 1) + pb + 1
+                        kept = block * v_near[ja + 1, jb + 1, at:at + 1, :width]
+                        m_near[ja + 1, jb + 1, pa + 1, pb + 1] = kept.astype(jnp.bfloat16)
+
+    complete(True)
     margin.finish()
+    complete(False)
     density.finish()
 
     def put_first(a, b, value):
@@ -197,6 +260,7 @@
         product(d_row, m_own, m_near, keep, put_first)
         if turn:
             rows.relay()
+            overlap(h_left, lambda ka, kb: w_near.at[ka + 1, kb + 1], width, put_ham)
             rows.finish()
 
         def put_third(a, b, value):
@@ -207,6 +271,8 @@
         cubic = halo(t_row, t_near)
         cubic.start()
         cubic.relay()
+        if not turn:
+            prepare([(ka, kb) for ka in (-1, 1) for kb in SPAN])
         cubic.finish()
         started.append(cubic)
         after = nears[turn + 1][0].at[1, 1] if turn + 1 < len(nears) else None
@@ -228,34 +294,31 @@
 
 def body(counts, orbitals, potential, density, pattern):
     width, cells = orbitals.shape[3], orbitals.shape[4]
-    keep = jnp.broadcast_to(
-        pattern.reshape(3, 3, 1, 1).astype(jnp.float32), (3, 3, 1, 128)
-    )
     near = pltpu.VMEM((3, 3, 3, 3, width, width), jnp.bfloat16)
     blocks = jax.ShapeDtypeStruct((3, 3, width, width), jnp.float32)
     vmem = pl.BlockSpec(memory_space=pltpu.VMEM)
     outs = pl.pallas_call(
         functools.partial(kernel, counts),
         out_shape=(blocks,) * 3,
-        in_specs=[vmem] * 4,
+        in_specs=[vmem, vmem, vmem, pl.BlockSpec(memory_space=pltpu.SMEM)],
         out_specs=(vmem,) * 3,
         scratch_shapes=[
             pltpu.VMEM((3, 3, 3, 3, width, cells), jnp.bfloat16),
-            pltpu.VMEM((3, 3, 1, 1, cells), jnp.float32),
+            pltpu.VMEM((3, 3, 16, cells), jnp.float32),
             pltpu.VMEM((3, 3, 3, 3, width, 2 * cells), jnp.bfloat16),
-            near, near, near, near, near,
+            near, near, near, near, near, near,
             pltpu.VMEM((3, 3, width, width), jnp.bfloat16),
-            pltpu.SemaphoreType.DMA((7, 8)),
-            pltpu.SemaphoreType.DMA((7, 8)),
+            pltpu.SemaphoreType.DMA((7, 16)),
+            pltpu.SemaphoreType.DMA((7, 16)),
         ],
         compiler_params=pltpu.CompilerParams(
-            collective_id=0, has_side_effects=True, vmem_limit_bytes=60 * 2**20
+            collective_id=0, has_side_effects=True, vmem_limit_bytes=44 * 2**20
         ),
     )(
         orbitals.reshape(3, 3, width, cells),
         potential.reshape(1, 1, cells),
         density.reshape(3, 3, width, width),
-        keep,
+        pattern.reshape(9),
     )
     return tuple(out.reshape(1, 1, 9, width, width) for out in outs)
 

time: 116 us -> 99.7 us (0.86)
  Pallas kernels: 110 us -> 93.7 us
    pallas_call x1, Pallas kernels: 110 us -> 93.7 us  [body(): pl.pallas_call(functools.partial(kernel, counts), out_shape=(blocks,) * 3...]
    unnamed x9 -> x11, local copies, waits for them, and re-layouts: 4.72 us -> 5.14 us
where the time goes in v2:
time: 99.7 us; the launch traced here: 99.5 us
  Pallas kernels  93.7 us (94%)
  local copies, waits for them, and re-layouts  5.14 us (5%)
    pallas_call x1, Pallas kernels, body(): pl.pallas_call(functools.partial(kernel, counts), out_shape=(blocks,) * 3...  93.7 us
    unnamed x11, local copies, waits for them, and re-layouts  5.14 us

profile of v2, /device:TPU:1, one launch (start us, length us, event | category | flops | bytes accessed | tf_op | source)
XLA Modules:
  0.0 99.5 jit_solution(11707601933339187584)
XLA Ops:
  0.6 0.0 copy-start.2
  0.6 0.0 copy-start.3
  0.7 0.7 copy-done.2
  1.3 0.0 copy-done.3
  1.3 0.0 copy-start
  1.3 1.1 %copy-done = bf16[1,1,9,128,256]{4,3,2,1,0:T(8,128)(2,1)S(1)} copy-done((bf16[1,1,9,128,256]{4,3,2,1,0:T(8,128)(2,1)S(1)}, bf16[1,1,9,128,256]{4,3,2,1,0:T(8,128)(2,1)}, u32[]{:S(2)}) %copy-start) | copy-done | bytes 589848
  2.4 0.0 copy-start.1
  2.4 1.0 copy-done.1
  3.3 93.7 %shard_map.67 = (f32[3,3,128,128]{3,2,1,0:T(8,128)S(1)}, f32[3,3,128,128]{3,2,1,0:T(8,128)S(1)}, f32[3,3,128,128]{3,2,1,0:T(8,128)S(1)}) custom-call(bf16[3,3,128,256]{3,2,1,0:T(8,128)(2,1)S(1)} %bitcast.9, f32[1,1,256]{2,1,0:T(1,128)S(1)} %copy-done.2, bf16[3,3,128,128]{3,2,1,0:T(8,128)(2,1)S(1)} %bitcast.10, s32[9]{0:T(128)S(1)} %bitcast.11), custom_call_target="tpu_custom_call" | custom-call | tf_op jit(solution)/shard_map/pallas_call | solution.py:300
  97.0 0.8 copy.10
  97.9 0.8 copy.11
  98.7 0.8 copy.12
Async XLA Ops:
  0.6 0.7 copy-start.2
  0.6 0.7 copy-start.3
  1.3 1.1 %copy-start = (bf16[1,1,9,128,256]{4,3,2,1,0:T(8,128)(2,1)S(1)}, bf16[1,1,9,128,256]{4,3,2,1,0:T(8,128)(2,1)}, u32[]{:S(2)}) copy-start(bf16[1,1,9,128,256]{4,3,2,1,0:T(8,128)(2,1)} %param.4) | copy-start | bytes 1769476
  2.4 1.0 copy-start.1
